TPU v7x, 32 devices: a whole 2x2x4 slice. The times are simulated.
32 devices in a mesh: ctx: 32 (over z, y, x, core).
Axes of the slice: x: 2, y: 2, z: 4, core: 2. Of those that a mesh axis runs over, the one named last changes fastest.
Arguments:
- query: bfloat16 [4096, 1024], P('ctx'), may hold values from -11 to 11
- key: bfloat16 [4096, 128], P('ctx'), may hold values from -4 to 4
- value: bfloat16 [4096, 128], P('ctx'), may hold values from -4 to 4
- out_grad: bfloat16 [4096, 1024], P('ctx'), may hold values from -4 to 4
- lengths: int32 [32], replicated, may hold values from 1 to 1409, 4096 in all
Outputs:
- attended: bfloat16 [4096, 1024], P('ctx')
- grad_query: bfloat16 [4096, 1024], P('ctx')
- grad_key: bfloat16 [4096, 128], P('ctx')
- grad_value: bfloat16 [4096, 128], P('ctx')
Inputs may be any that keep to these rules, and one draw needn't show every extreme that they name: The lengths of the 32 documents in order; they sum to 4096.
All inputs are finite; a program needn't handle non-finite values.
Results may differ from a plain program's by a relative error of at most 0.03.
Values may be sent and summed in bfloat16 or wider, within the bound.
A program may use at most 64 MiB of HBM per device.

v0:
```python
import math

import jax
import jax.numpy as jnp
from jax import lax
from jax.sharding import PartitionSpec as P

SPAN = 11


def from_behind(value, axis, steps):
    count = lax.axis_size(axis)
    first, last = (max(0, -steps), min(count, count - steps))
    return lax.ppermute(value, axis, [(source, source + steps) for source in range(first, last)])


def visible(query_pos, starts, key_slice):
    return (key_slice[None, :] >= starts[:, None]) & (key_slice[None, :] <= query_pos[:, None])


def body(query, key, value, out_grad, lengths):
    tok_count = query.shape[0]
    head_dim = key.shape[1]
    head_count = query.shape[1] // head_dim
    slot_count = SPAN + 1
    scaling = head_dim ** (-0.5)
    my_index = lax.axis_index("ctx")
    key_value = jnp.stack([key, value])
    gathered = key_value[None]
    levels = []
    filled = 1
    while filled < slot_count:
        taken = min(filled, slot_count - filled)
        arrived = from_behind(gathered[:taken], "ctx", filled)
        gathered = jnp.concatenate([gathered, arrived], 0)
        levels.append((filled, taken))
        filled += taken
    span_keys = slot_count * tok_count
    keys_all = gathered[:, 0].reshape(span_keys, head_dim)
    values_all = gathered[:, 1].reshape(span_keys, head_dim)
    offsets = jnp.arange(tok_count, dtype=jnp.int32)
    query_pos = my_index * tok_count + offsets
    slot_ids = jnp.arange(slot_count, dtype=jnp.int32)
    key_pos = ((my_index - slot_ids)[:, None] * tok_count + offsets[None, :]).reshape(-1)
    doc_ends = jnp.cumsum(lengths)
    starts = jnp.max(
        jnp.where(doc_ends[None, :] <= query_pos[:, None], doc_ends[None, :], 0), axis=1
    )
    queries = query.reshape(tok_count, head_count, head_dim)
    grads_out = out_grad.reshape(tok_count, head_count, head_dim)
    key_step = math.gcd(span_keys, 256)
    step_count = span_keys // key_step

    def scores_at(block_index):
        begin = block_index * key_step
        key_block = lax.dynamic_slice_in_dim(keys_all, begin, key_step, 0)
        value_block = lax.dynamic_slice_in_dim(values_all, begin, key_step, 0)
        key_slice = lax.dynamic_slice_in_dim(key_pos, begin, key_step, 0)
        allowed = visible(query_pos, starts, key_slice)
        logits = (
            jnp.einsum("thc,kc->htk", queries, key_block, preferred_element_type=jnp.float32)
            * scaling
        )
        return (key_block, value_block, allowed, jnp.where(allowed[None], logits, -1e30))

    def gather_stats(block_index, running):
        row_max, row_sum = running
        _, _, allowed, scores = scores_at(block_index)
        new_max = jnp.maximum(row_max, jnp.max(scores, axis=2))
        fresh = jnp.sum(jnp.where(allowed[None], jnp.exp(scores - new_max[..., None]), 0.0), axis=2)
        return (new_max, row_sum * jnp.exp(row_max - new_max) + fresh)

    stats_start = (
        jnp.full((head_count, tok_count), -1e30, jnp.float32),
        jnp.zeros((head_count, tok_count), jnp.float32),
    )
    row_max, row_sum = lax.fori_loop(0, step_count, gather_stats, stats_start)

    def probs_at(allowed, scores):
        return jnp.where(
            allowed[None], jnp.exp(scores - row_max[..., None]) / row_sum[..., None], 0.0
        )

    def forward_step(block_index, summed):
        _, value_block, allowed, scores = scores_at(block_index)
        weights = probs_at(allowed, scores).astype(jnp.bfloat16)
        return summed + jnp.einsum(
            "htk,kc->thc", weights, value_block, preferred_element_type=jnp.float32
        )

    summed_out = lax.fori_loop(
        0, step_count, forward_step, jnp.zeros((tok_count, head_count, head_dim), jnp.float32)
    )
    attended = summed_out.astype(jnp.bfloat16)
    row_dot = jnp.einsum("thc,thc->ht", grads_out.astype(jnp.float32), attended.astype(jnp.float32))

    def backward_step(block_index, running):
        query_sum, grad_window = running
        key_block, value_block, allowed, scores = scores_at(block_index)
        probabilities = probs_at(allowed, scores)
        weights = probabilities.astype(jnp.bfloat16)
        grad_probs = jnp.einsum(
            "thc,kc->htk", grads_out, value_block, preferred_element_type=jnp.float32
        )
        grad_scores = (probabilities * (grad_probs - row_dot[..., None])).astype(jnp.bfloat16)
        query_sum = query_sum + jnp.einsum(
            "htk,kc->thc", grad_scores, key_block, preferred_element_type=jnp.float32
        )
        key_term = (
            jnp.einsum("htk,thc->kc", grad_scores, queries, preferred_element_type=jnp.float32)
            * scaling
        )
        value_term = jnp.einsum(
            "htk,thc->kc", weights, grads_out, preferred_element_type=jnp.float32
        )
        grad_window = lax.dynamic_update_slice_in_dim(
            grad_window, jnp.stack([key_term, value_term]), block_index * key_step, 1
        )
        return (query_sum, grad_window)

    backward_start = (
        jnp.zeros((tok_count, head_count, head_dim), jnp.float32),
        jnp.zeros((2, span_keys, head_dim), jnp.float32),
    )
    query_sum, grad_window = lax.fori_loop(0, step_count, backward_step, backward_start)
    grad_query = (
        (query_sum * scaling).astype(jnp.bfloat16).reshape(tok_count, head_count * head_dim)
    )
    window_grads = grad_window.reshape(2, slot_count, tok_count, head_dim)
    for filled, taken in reversed(levels):
        arrived = from_behind(window_grads[:, filled : filled + taken], "ctx", -filled)
        window_grads = window_grads[:, :filled].at[:, :taken].add(arrived)
    owned = window_grads[:, 0]
    attended_flat = attended.reshape(tok_count, head_count * head_dim)
    return (attended_flat, grad_query, owned[0].astype(jnp.bfloat16), owned[1].astype(jnp.bfloat16))


def solution(mesh):
    placed = (P("ctx", None), P("ctx", None), P("ctx", None), P("ctx", None), P())
    return jax.shard_map(
        body,
        mesh=mesh,
        in_specs=placed,
        out_specs=(P("ctx", None), P("ctx", None), P("ctx", None), P("ctx", None)),
        check_vma=False,
    )
```

profile of v0, /device:TPU:21, one launch (start us, length us, event | category | flops | bytes accessed | tf_op | source)
XLA Modules:
  0.0 91.2 jit_solution(15292880503617317860)
XLA Ops:
  0.6 0.8 maximum_bitcast_fusion
  1.5 3.7 %collective-permute-start = (bf16[1,2,128,128]{3,2,1,0:T(8,128)(2,1)S(1)}, bf16[1,2,128,128]{3,2,1,0:T(8,128)(2,1)S(1)}, u32[]{:S(2)}, u32[]{:S(2)}) collective-permute-start(bf16[1,2,128,128]{3,2,1,0:T(8,128)(2,1)S(1)} %maximum_bitcast_fusion), channel_id=1, source_target_pairs={{0,1},{1,2},{2,3},{3,4},{4,5},{5,6},{6,7},{7,8},{8,9},{9,10},{10,1... | collective-permute-start | bytes 196616 | tf_op jit(solution)/shard_map/ppermute | solution.py:14
  5.2 1.2 %collective-permute-done = bf16[1,2,128,128]{3,2,1,0:T(8,128)(2,1)S(1)} collective-permute-done((bf16[1,2,128,128]{3,2,1,0:T(8,128)(2,1)S(1)}, bf16[1,2,128,128]{3,2,1,0:T(8,128)(2,1)S(1)}, u32[]{:S(2)}, u32[]{:S(2)}) %collective-permute-start) | collective-permute-done | bytes 65568 | tf_op jit(solution)/shard_map/ppermute | solution.py:14
  6.5 3.1 %collective-permute-start.1 = (bf16[2,2,128,128]{3,2,1,0:T(8,128)(2,1)S(1)}, bf16[2,2,128,128]{3,2,1,0:T(8,128)(2,1)S(1)}, u32[]{:S(2)}, u32[]{:S(2)}) collective-permute-start(bf16[2,2,128,128]{3,2,1,0:T(8,128)(2,1)S(1)} %pad_maximum_fusion.1), channel_id=1, source_target_pairs={{0,2},{1,3},{2,4},{3,5},{4,6},{5,7},{6,8},{7,9},{8,10},{9,11},{10,... | collective-permute-start | bytes 393224 | tf_op jit(solution)/shard_map/ppermute | solution.py:14
  9.6 0.7 copy.31
  10.5 0.8 constant_dynamic-update-slice_fusion.4
  11.3 1.8 %collective-permute-done.1 = bf16[2,2,128,128]{3,2,1,0:T(8,128)(2,1)S(1)} collective-permute-done((bf16[2,2,128,128]{3,2,1,0:T(8,128)(2,1)S(1)}, bf16[2,2,128,128]{3,2,1,0:T(8,128)(2,1)S(1)}, u32[]{:S(2)}, u32[]{:S(2)}) %collective-permute-start.1) | collective-permute-done | bytes 131104 | tf_op jit(solution)/shard_map/ppermute | solution.py:14
  13.1 4.0 %collective-permute-start.2 = (bf16[4,2,128,128]{3,2,1,0:T(8,128)(2,1)S(1)}, bf16[4,2,128,128]{3,2,1,0:T(8,128)(2,1)S(1)}, u32[]{:S(2)}, u32[]{:S(2)}) collective-permute-start(bf16[4,2,128,128]{3,2,1,0:T(8,128)(2,1)S(1)} %pad_maximum_fusion), channel_id=1, source_target_pairs={{0,4},{1,5},{2,6},{3,7},{4,8},{5,9},{6,10},{7,11},{8,12},{9,13},{1... | collective-permute-start | bytes 786440 | tf_op jit(solution)/shard_map/ppermute | solution.py:14
  17.3 1.1 %copy.37 = bf16[128,1024]{0,1:T(8,128)(2,1)S(1)} copy(bf16[128,1024]{1,0:T(8,128)(2,1)} %param.28) | data formatting | bytes 524288 | tf_op args[3]
  19.0 1.9 %collective-permute-start.3 = (bf16[4,2,128,128]{3,2,1,0:T(8,128)(2,1)S(1)}, bf16[4,2,128,128]{3,2,1,0:T(8,128)(2,1)S(1)}, u32[]{:S(2)}, u32[]{:S(2)}) collective-permute-start(bf16[4,2,128,128]{3,2,1,0:T(8,128)(2,1)S(1)} %pad_maximum_fusion), channel_id=1, source_target_pairs={{0,8},{1,9},{2,10},{3,11},{4,12},{5,13},{6,14},{7,15},{8,16},{9,17... | collective-permute-start | bytes 786440 | tf_op jit(solution)/shard_map/ppermute | solution.py:14
  21.0 8.1 %collective-permute-done.3 = bf16[4,2,128,128]{3,2,1,0:T(8,128)(2,1)S(1)} collective-permute-done((bf16[4,2,128,128]{3,2,1,0:T(8,128)(2,1)S(1)}, bf16[4,2,128,128]{3,2,1,0:T(8,128)(2,1)S(1)}, u32[]{:S(2)}, u32[]{:S(2)}) %collective-permute-start.3) | collective-permute-done | bytes 262176 | tf_op jit(solution)/shard_map/ppermute | solution.py:14
  29.3 4.7 %while.53 = (s32[]{:T(128)}, f32[8,128]{1,0:T(8,128)S(1)}, f32[8,128]{1,0:T(8,128)S(1)}, s32[1536]{0:T(1024)S(1)}, s32[128]{0:T(128)S(1)}, /*index=5*/bf16[1536,...) while((s32[]{:T(128)}, f32[8,128]{1,0:T(8,128)S(1)}, ...), condition=%wide.region_5.6_spmd.clone, body=%wide.region_2.5_spmd.clone.sunk | while | flops 68785288 | bytes 2581186 | solution.py:77
  34.0 5.2 %while.54 = (s32[]{:T(128)}, f32[128,8,128]{0,2,1:T(8,128)S(1)}, bf16[1536,128]{1,0:T(8,128)(2,1)S(1)}, s32[1536]{0:T(1024)S(1)}, s32[128]{0:T(128)S(1)}, /*inde...) while((s32[]{:T(128)}, f32[128,8,128]{0,2,1:T(8,128)S(1)}, ...), condition=%wide.region_7.8_spmd.clone, body=%wide.region_6.7_spmd.clone.sunk | while | flops 136151168 | bytes 1521868 | solution.py:91
  34.2 0.6 fusion.102
  35.1 0.6 fusion.102
  35.9 0.6 fusion.102
  36.8 0.6 fusion.102
  37.7 0.6 fusion.102
  38.6 0.6 fusion.102
  39.2 0.8 fusion.62
  40.1 11.5 %while.55 = (s32[]{:T(128)}, f32[128,8,128]{0,2,1:T(8,128)S(1)}, f32[2,1536,128]{2,1,0:T(8,128)S(1)}, bf16[1536,128]{1,0:T(8,128)(2,1)S(1)}, s32[1536]{0:T(1024)...) while((s32[]{:T(128)}, f32[128,8,128]{0,2,1:T(8,128)S(1)}, ...), condition=%wide.region_9.10_spmd.clone, body=%wide.region_8.9_spmd.clone.sunk | while | flops 338362496 | bytes 7881461 | solution.py:125
  51.7 2.2 %collective-permute-start.4 = (f32[2,4,128,128]{3,2,1,0:T(8,128)S(1)}, f32[2,4,128,128]{3,2,1,0:T(8,128)S(1)}, u32[]{:S(2)}, u32[]{:S(2)}) collective-permute-start(f32[2,4,128,128]{3,2,1,0:T(8,128)S(1)} %get-tuple-element.854), channel_id=1, source_target_pairs={{8,0},{9,1},{10,2},{11,3},{12,4},{13,5},{14,6},{15,7},{16,8},{17,9... | collective-permute-start | bytes 1572872 | tf_op jit(solution)/shard_map/ppermute | solution.py:14
  53.9 1.9 %collective-permute-start.5 = (f32[2,4,128,128]{3,2,1,0:T(8,128)S(1)}, f32[2,4,128,128]{3,2,1,0:T(8,128)S(1)}, u32[]{:S(2)}, u32[]{:S(2)}) collective-permute-start(f32[2,4,128,128]{3,2,1,0:T(8,128)S(1)} %get-tuple-element.855), channel_id=1, source_target_pairs={{4,0},{5,1},{6,2},{7,3},{8,4},{9,5},{10,6},{11,7},{12,8},{13,9},{1... | collective-permute-start | bytes 1572872 | tf_op jit(solution)/shard_map/ppermute | solution.py:14
  55.8 8.5 %collective-permute-done.4 = f32[2,4,128,128]{3,2,1,0:T(8,128)S(1)} collective-permute-done((f32[2,4,128,128]{3,2,1,0:T(8,128)S(1)}, f32[2,4,128,128]{3,2,1,0:T(8,128)S(1)}, u32[]{:S(2)}, u32[]{:S(2)}) %collective-permute-start.4) | collective-permute-done | bytes 524320 | tf_op jit(solution)/shard_map/ppermute | solution.py:14
  64.3 6.3 %collective-permute-done.5 = f32[2,4,128,128]{3,2,1,0:T(8,128)S(1)} collective-permute-done((f32[2,4,128,128]{3,2,1,0:T(8,128)S(1)}, f32[2,4,128,128]{3,2,1,0:T(8,128)S(1)}, u32[]{:S(2)}, u32[]{:S(2)}) %collective-permute-start.5) | collective-permute-done | bytes 524320 | tf_op jit(solution)/shard_map/ppermute | solution.py:14
  70.8 1.9 %collective-permute-start.6 = (f32[2,2,128,128]{3,2,1,0:T(8,128)S(1)}, f32[2,2,128,128]{3,2,1,0:T(8,128)S(1)}, u32[]{:S(2)}, u32[]{:S(2)}) collective-permute-start(f32[2,2,128,128]{3,2,1,0:T(8,128)S(1)} %slice.156), channel_id=1, source_target_pairs={{2,0},{3,1},{4,2},{5,3},{6,4},{7,5},{8,6},{9,7},{10,8},{11,9},{12,... | collective-permute-start | bytes 786440 | tf_op jit(solution)/shard_map/ppermute | solution.py:14
  72.7 0.9 copy.50
  73.5 4.3 %collective-permute-done.6 = f32[2,2,128,128]{3,2,1,0:T(8,128)S(1)} collective-permute-done((f32[2,2,128,128]{3,2,1,0:T(8,128)S(1)}, f32[2,2,128,128]{3,2,1,0:T(8,128)S(1)}, u32[]{:S(2)}, u32[]{:S(2)}) %collective-permute-start.6) | collective-permute-done | bytes 262176 | tf_op jit(solution)/shard_map/ppermute | solution.py:14
  77.9 8.0 %collective-permute-start.7 = (f32[2,1,128,128]{3,2,1,0:T(8,128)S(1)}, f32[2,1,128,128]{3,2,1,0:T(8,128)S(1)}, u32[]{:S(2)}, u32[]{:S(2)}) collective-permute-start(f32[2,1,128,128]{3,2,1,0:T(8,128)S(1)} %slice.158), channel_id=1, source_target_pairs={{1,0},{2,1},{3,2},{4,3},{5,4},{6,5},{7,6},{8,7},{9,8},{10,9},{11,1... | collective-permute-start | bytes 393224 | tf_op jit(solution)/shard_map/ppermute | solution.py:14
  86.0 0.9 copy.53
  86.8 3.7 %collective-permute-done.7 = f32[2,1,128,128]{3,2,1,0:T(8,128)S(1)} collective-permute-done((f32[2,1,128,128]{3,2,1,0:T(8,128)S(1)}, f32[2,1,128,128]{3,2,1,0:T(8,128)S(1)}, u32[]{:S(2)}, u32[]{:S(2)}) %collective-permute-start.7) | collective-permute-done | bytes 131104 | tf_op jit(solution)/shard_map/ppermute | solution.py:14
  90.6 0.6 slice_bitcast_fusion
  (155 shorter events, 17.9 us)
Async XLA Ops:
  0.6 18.0 %copy-start.2 = (bf16[128,1024]{1,0:T(8,128)(2,1)S(1)}, bf16[128,1024]{1,0:T(8,128)(2,1)}, u32[]{:S(2)}) copy-start(bf16[128,1024]{1,0:T(8,128)(2,1)} %param.25) | copy-start | bytes 786436
  1.5 5.0 %collective-permute-start = (bf16[1,2,128,128]{3,2,1,0:T(8,128)(2,1)S(1)}, bf16[1,2,128,128]{3,2,1,0:T(8,128)(2,1)S(1)}, u32[]{:S(2)}, u32[]{:S(2)}) collective-permute-start(bf16[1,2,128,128]{3,2,1,0:T(8,128)(2,1)S(1)} %maximum_bitcast_fusion), channel_id=1, source_target_pairs={{0,1},{1,2},{2,3},{3,4},{4,5},{5,6},{6,7},{7,8},{8,9},{9,10},{10,1... | collective-permute-start | bytes 196616 | tf_op jit(solution)/shard_map/ppermute | solution.py:14
  6.5 6.6 %collective-permute-start.1 = (bf16[2,2,128,128]{3,2,1,0:T(8,128)(2,1)S(1)}, bf16[2,2,128,128]{3,2,1,0:T(8,128)(2,1)S(1)}, u32[]{:S(2)}, u32[]{:S(2)}) collective-permute-start(bf16[2,2,128,128]{3,2,1,0:T(8,128)(2,1)S(1)} %pad_maximum_fusion.1), channel_id=1, source_target_pairs={{0,2},{1,3},{2,4},{3,5},{4,6},{5,7},{6,8},{7,9},{8,10},{9,11},{10,... | collective-permute-start | bytes 393224 | tf_op jit(solution)/shard_map/ppermute | solution.py:14
  13.1 7.8 %collective-permute-start.2 = (bf16[4,2,128,128]{3,2,1,0:T(8,128)(2,1)S(1)}, bf16[4,2,128,128]{3,2,1,0:T(8,128)(2,1)S(1)}, u32[]{:S(2)}, u32[]{:S(2)}) collective-permute-start(bf16[4,2,128,128]{3,2,1,0:T(8,128)(2,1)S(1)} %pad_maximum_fusion), channel_id=1, source_target_pairs={{0,4},{1,5},{2,6},{3,7},{4,8},{5,9},{6,10},{7,11},{8,12},{9,13},{1... | collective-permute-start | bytes 786440 | tf_op jit(solution)/shard_map/ppermute | solution.py:14
  19.0 10.2 %collective-permute-start.3 = (bf16[4,2,128,128]{3,2,1,0:T(8,128)(2,1)S(1)}, bf16[4,2,128,128]{3,2,1,0:T(8,128)(2,1)S(1)}, u32[]{:S(2)}, u32[]{:S(2)}) collective-permute-start(bf16[4,2,128,128]{3,2,1,0:T(8,128)(2,1)S(1)} %pad_maximum_fusion), channel_id=1, source_target_pairs={{0,8},{1,9},{2,10},{3,11},{4,12},{5,13},{6,14},{7,15},{8,16},{9,17... | collective-permute-start | bytes 786440 | tf_op jit(solution)/shard_map/ppermute | solution.py:14
  29.3 4.7 %copy-start.1 = (f32[128,8,128]{0,2,1:T(8,128)S(1)}, f32[128,8,128]{0,2,1:T(8,128)}, u32[]{:S(2)}) copy-start(f32[128,8,128]{0,2,1:T(8,128)} %custom-call.2) | copy-start | bytes 1572868
  51.7 21.0 %copy-start = (bf16[128,8,128]{0,2,1:T(8,128)(2,1)S(1)}, bf16[128,8,128]{0,2,1:T(8,128)(2,1)}, u32[]{:S(2)}) copy-start(bf16[128,8,128]{0,2,1:T(8,128)(2,1)} %get-tuple-element.851) | copy-start | bytes 786436
  51.7 12.6 %collective-permute-start.4 = (f32[2,4,128,128]{3,2,1,0:T(8,128)S(1)}, f32[2,4,128,128]{3,2,1,0:T(8,128)S(1)}, u32[]{:S(2)}, u32[]{:S(2)}) collective-permute-start(f32[2,4,128,128]{3,2,1,0:T(8,128)S(1)} %get-tuple-element.854), channel_id=1, source_target_pairs={{8,0},{9,1},{10,2},{11,3},{12,4},{13,5},{14,6},{15,7},{16,8},{17,9... | collective-permute-start | bytes 1572872 | tf_op jit(solution)/shard_map/ppermute | solution.py:14
  53.9 16.7 %collective-permute-start.5 = (f32[2,4,128,128]{3,2,1,0:T(8,128)S(1)}, f32[2,4,128,128]{3,2,1,0:T(8,128)S(1)}, u32[]{:S(2)}, u32[]{:S(2)}) collective-permute-start(f32[2,4,128,128]{3,2,1,0:T(8,128)S(1)} %get-tuple-element.855), channel_id=1, source_target_pairs={{4,0},{5,1},{6,2},{7,3},{8,4},{9,5},{10,6},{11,7},{12,8},{13,9},{1... | collective-permute-start | bytes 1572872 | tf_op jit(solution)/shard_map/ppermute | solution.py:14
  70.8 7.1 %collective-permute-start.6 = (f32[2,2,128,128]{3,2,1,0:T(8,128)S(1)}, f32[2,2,128,128]{3,2,1,0:T(8,128)S(1)}, u32[]{:S(2)}, u32[]{:S(2)}) collective-permute-start(f32[2,2,128,128]{3,2,1,0:T(8,128)S(1)} %slice.156), channel_id=1, source_target_pairs={{2,0},{3,1},{4,2},{5,3},{6,4},{7,5},{8,6},{9,7},{10,8},{11,9},{12,... | collective-permute-start | bytes 786440 | tf_op jit(solution)/shard_map/ppermute | solution.py:14
  77.9 12.6 %collective-permute-start.7 = (f32[2,1,128,128]{3,2,1,0:T(8,128)S(1)}, f32[2,1,128,128]{3,2,1,0:T(8,128)S(1)}, u32[]{:S(2)}, u32[]{:S(2)}) collective-permute-start(f32[2,1,128,128]{3,2,1,0:T(8,128)S(1)} %slice.158), channel_id=1, source_target_pairs={{1,0},{2,1},{3,2},{4,3},{5,4},{6,5},{7,6},{8,7},{9,8},{10,9},{11,1... | collective-permute-start | bytes 393224 | tf_op jit(solution)/shard_map/ppermute | solution.py:14
where the time goes:
time: 91.6 us; the launch traced here: 91.2 us
  waiting for transfers between devices  34 us (37%)
  starting transfers between devices  26.8 us (29%)
  matrix products  15.4 us (17%)
  local copies, waits for them, and re-layouts  6.57 us (7%)
  other arithmetic  6.3 us (7%)
  loops' own time  1.18 us (1%)
  between operations  0.94 us (1%)
    ppermute x8, waiting for transfers between devices, from_behind(): lax.ppermute(value, axis, [(source, source + steps) for source in range(f...  34 us
    ppermute x8, starting transfers between devices, from_behind(): lax.ppermute(value, axis, [(source, source + steps) for source in range(f...  26.8 us
    dot_general x12, matrix products, scores_at(): jnp.einsum('thc,kc->htk', queries, key_block, preferred_element_type=jnp....  4.46 us
    dot_general x6, matrix products, forward_step(): jnp.einsum('htk,kc->thc', weights, value_block, preferred_element_type=jn...  3.81 us
    dot_general x6, matrix products, backward_step(): jnp.einsum('htk,kc->thc', grad_scores, key_block, preferred_element_type=...  1.92 us
    and x18, other arithmetic, visible(): (key_slice[None, :] >= starts[:, None]) & (key_slice[None, :] <= query_po...  1.87 us
  transfers between devices with their start and end apart: 8, of which 7 were waited for; matrix products, arithmetic and copies ran while one was open for 6% of the time, Pallas kernels for 0%

commit v1 on v0

v1 whole, which is shorter than its diff:
```python
import functools

import jax
import jax.numpy as jnp
from jax import lax
from jax.experimental import pallas as pl
from jax.experimental.pallas import tpu as pltpu
from jax.sharding import PartitionSpec as P

SPAN = 11
SLOTS = SPAN + 1
GROUP = 8
LOG2E = 1.4426950408889634
MESH = pl.DeviceIdType.MESH

FORWARD_CHUNKS = ((0,), (8, 2), (4, 6), (1, 3), (5, 7), (10, 9), (11,))
BACKWARD_ORDER = (10, 2, 0, 4, 6, 8)


def contract(a, b, dims):
    return lax.dot_general(a, b, (dims, ((), ())), preferred_element_type=jnp.float32)


def kernel(
    count,
    lengths, query, key, value, out_grad,
    attended, grad_query, grad_key, grad_value,
    q, g, g_t, kv, e_all, dp_all, m_slot, m_run, l_run, o_t, dq_t,
    part, outbox, partner_in, own_in, fwd_in, far_in, att_buf, dq_buf, dkv_buf,
    load_sem, recv_sem, send_sem, grad_recv, grad_send, out_sem,
):
    tok = key.shape[0]
    hd = key.shape[1]
    heads = query.shape[1] // hd
    wide = 2 * hd
    rows = heads * tok
    pairs = heads // 2
    scale = hd ** -0.5
    me = lax.axis_index("ctx")
    place = lax.rem(me, GROUP)
    chip = place // 2
    odd = lax.rem(me, 2)
    is_even = odd == 0
    is_odd = odd == 1
    partner = me + 1 - 2 * odd
    chips = GROUP // 2

    loads = [
        pltpu.make_async_copy(key, kv.at[0, 0], load_sem.at[0]),
        pltpu.make_async_copy(value, kv.at[0, 1], load_sem.at[1]),
    ]
    for h in range(heads):
        cols = pl.ds(h * hd, hd)
        at = pl.ds(h * tok, tok)
        loads.append(pltpu.make_async_copy(query.at[:, cols], q.at[at, :], load_sem.at[2 + 2 * h]))
        loads.append(pltpu.make_async_copy(out_grad.at[:, cols], g.at[at, :], load_sem.at[3 + 2 * h]))
    for copy in loads:
        copy.start()

    greet = [(partner, None)]
    for dh in range(1, chips):
        greet.append((me + 2 * dh, chip + dh < chips))
        greet.append((me - 2 * dh, chip - dh >= 0))
    greet.append((me + 2, (chip == chips - 1) & (me + 2 < count)))
    greet.append((me - 2, (chip == 0) & (me - 2 >= 0)))
    greet.append((me + GROUP, me + GROUP < count))
    greet.append((me - GROUP, me - GROUP >= 0))
    greet.append((me + 3, is_odd & (me + 3 < count)))
    greet.append((me - 3, is_even & (me - 3 >= 0)))
    barrier = pltpu.get_barrier_semaphore()
    total = jnp.int32(1)
    for device, there in greet:
        if there is None:
            pl.semaphore_signal(barrier, inc=1, device_id=(device,), device_id_type=MESH)
        else:
            @pl.when(there)
            def _(device=device):
                pl.semaphore_signal(barrier, inc=1, device_id=(device,), device_id_type=MESH)
            total = total + there.astype(jnp.int32)
    loads[0].wait()
    loads[1].wait()
    pl.semaphore_wait(barrier, total)

    sent = []

    def send(src, dst, ssem, rsem, device, there):
        copy = pltpu.make_async_remote_copy(
            src_ref=src, dst_ref=dst, send_sem=ssem, recv_sem=rsem,
            device_id=(device,), device_id_type=MESH)

        @pl.when(there)
        def _():
            copy.start()
        sent.append((copy, there))

    n_send = [0]

    def send_slot(slot, dst_slot, device, there):
        k = n_send[0]
        n_send[0] += 1
        send(kv.at[slot], kv.at[dst_slot], send_sem.at[k], recv_sem.at[dst_slot], device, there)

    def arrive(slot):
        @pl.when(me >= slot)
        def _():
            pltpu.make_async_remote_copy(
                src_ref=kv.at[slot], dst_ref=kv.at[slot], send_sem=send_sem.at[0],
                recv_sem=recv_sem.at[slot], device_id=(partner,), device_id_type=MESH).wait_recv()

    def relay(slot):
        arrive(slot)
        send_slot(slot, slot + 1 - 2 * odd, partner, me >= slot)

    send_slot(0, GROUP, me + GROUP, me + GROUP < count)
    send_slot(0, 1, partner, is_even)
    for dh in range(1, chips):
        send_slot(0, 2 * dh, me + 2 * dh, chip + dh < chips)

    for slot in range(1, SLOTS):
        @pl.when(me < slot)
        def _(slot=slot):
            kv[slot] = jnp.zeros_like(kv[slot])
    lane_pos = me * tok + lax.broadcasted_iota(jnp.int32, (1, tok), 1)

    def doc_step(d, carry):
        end, start = carry
        end = end + lengths[d]
        return end, jnp.where(end <= lane_pos, end, start)

    _, start = lax.fori_loop(
        0, lengths.shape[0], doc_step, (jnp.int32(0), jnp.zeros((1, tok), jnp.int32)))
    for copy in loads[2:]:
        copy.wait()
    for h in range(heads):
        at = pl.ds(h * tok, tok)
        g_t[:, at] = jnp.transpose(g[at, :].astype(jnp.float32))

    def forward(slots, first):
        biases = []
        for slot in slots:
            key_pos = (me - slot) * tok + lax.broadcasted_iota(jnp.int32, (tok, 1), 0)
            seen = key_pos >= start
            if slot == 0:
                seen = seen & (key_pos <= lane_pos)
            biases.append(jnp.where(seen, 0.0, -1e30).astype(jnp.float32))
        bias = jnp.concatenate(biases, 0) if len(slots) > 1 else biases[0]
        bias = jnp.concatenate([bias, bias], 1)
        kb = jnp.concatenate([kv[s, 0] for s in slots], 0)
        vb = jnp.concatenate([kv[s, 1] for s in slots], 0)
        for hp in range(pairs):
            at = pl.ds(hp * 2 * tok, 2 * tok)
            s = contract(kb, q[at, :], ((1,), (1,))) * (scale * LOG2E) + bias
            dp = contract(vb, g[at, :], ((1,), (1,)))
            top = jnp.max(s, axis=0, keepdims=True)
            if not first:
                old = m_run[:, at]
                top = jnp.maximum(old, top)
            e = jnp.exp2(s - top)
            fresh = jnp.sum(e, axis=0, keepdims=True)
            o = contract(vb, e.astype(jnp.bfloat16), ((0,), (0,)))
            if first:
                l_run[:, at] = fresh
                o_t[:, at] = o
            else:
                alpha = jnp.exp2(old - top)
                l_run[:, at] = l_run[:, at] * alpha + fresh
                o_t[:, at] = o_t[:, at] * alpha + o
            m_run[:, at] = top
            for n, slot in enumerate(slots):
                e_all[slot, :, at] = e[n * tok:(n + 1) * tok]
                dp_all[slot, :, at] = dp[n * tok:(n + 1) * tok]
                m_slot[slot, :, at] = top

    forward((0,), True)
    arrive(GROUP)
    have = me >= GROUP
    send_slot(GROUP, GROUP + 2, me + 2, have & (me + 2 < count))
    for dh in range(1, chips):
        send_slot(GROUP, GROUP - 2 * dh, me - 2 * dh, have & (chip - dh >= 0))
    send_slot(GROUP, GROUP + 3, me + 3, have & is_odd & (me + 3 < count))
    send_slot(GROUP, GROUP + 1 - 2 * odd, partner, have)
    relay(2)
    forward((8, 2), False)
    relay(4)
    relay(6)
    forward((4, 6), False)
    relay(10)
    arrive(1)
    arrive(3)
    forward((1, 3), False)
    arrive(5)
    arrive(7)
    forward((5, 7), False)
    arrive(9)
    forward((10, 9), False)
    arrive(11)
    forward((11,), False)

    inv = 1.0 / l_run[...]
    att = (o_t[...] * inv).astype(jnp.bfloat16).astype(jnp.float32)
    o_t[...] = att
    row_dot = jnp.sum(g_t[...] * att, axis=0, keepdims=True)
    m_end = m_run[...]

    def chunk(i):
        e_slot = BACKWARD_ORDER[i]
        o_slot = lax.rem(e_slot + 2 * odd - 1 + SLOTS, SLOTS)
        slots = (e_slot, o_slot)
        kb = jnp.concatenate([kv[s, 0] for s in slots], 0)
        dk = jnp.zeros((2 * tok, hd), jnp.float32)
        dv = jnp.zeros((2 * tok, hd), jnp.float32)
        for hp in range(pairs):
            lo = hp * 2 * tok
            at = pl.ds(lo, 2 * tok)
            dot = row_dot[:, lo:lo + 2 * tok]
            ps, dss = [], []
            for s in slots:
                f = jnp.exp2(m_slot[s, :, at] - m_end[:, lo:lo + 2 * tok]) * inv[:, lo:lo + 2 * tok]
                p = e_all[s, :, at] * f
                dss.append((p * (dp_all[s, :, at] - dot)).astype(jnp.bfloat16))
                ps.append(p.astype(jnp.bfloat16))
            p = jnp.concatenate(ps, 0)
            ds = jnp.concatenate(dss, 0)
            dv = dv + contract(p, g[at, :], ((1,), (0,)))
            dk = dk + contract(ds, q[at, :], ((1,), (0,)))
            dq = contract(kb, ds, ((0,), (0,)))
            if i == 0:
                dq_t[:, at] = dq
            else:
                dq_t[:, at] = dq_t[:, at] + dq
        dk = dk * scale
        k = e_slot // 2
        part[k, 0] = dk[:tok]
        part[k, 1] = dv[:tok]
        outbox[k, 0] = dk[tok:].astype(jnp.bfloat16)
        outbox[k, 1] = dv[tok:].astype(jnp.bfloat16)
        if e_slot == 0:
            send(outbox.at[k], partner_in.at[0], grad_send.at[0], grad_recv.at[0], partner, is_odd)
            send(outbox.at[k], far_in.at[1], grad_send.at[1], grad_recv.at[15], me - 3,
                 is_even & (me >= SPAN))
        else:
            send(outbox.at[k], partner_in.at[k], grad_send.at[1 + k], grad_recv.at[k], partner,
                 me >= o_slot)

    def take(ref, sem, there, base):
        @pl.when(there)
        def _():
            pltpu.make_async_remote_copy(
                src_ref=ref, dst_ref=ref, send_sem=grad_send.at[0], recv_sem=sem,
                device_id=(partner,), device_id_type=MESH).wait_recv()
            part[base] = part[base] + ref[...].astype(jnp.float32)

    def up(e_slot):
        k = e_slot // 2
        take(partner_in.at[k], grad_recv.at[k], me >= e_slot, k)
        outbox[SLOTS // 2 + k] = part[k].astype(jnp.bfloat16)
        box = outbox.at[SLOTS // 2 + k]
        near = chip - k >= 0
        if e_slot < GROUP:
            send(box, own_in.at[k - 1], grad_send.at[6 + k], grad_recv.at[5 + k], me - e_slot, near)
            send(box, fwd_in.at[k - 1], grad_send.at[9 + k], grad_recv.at[8 + k],
                 me + GROUP - e_slot, jnp.logical_not(near) & (me >= e_slot))
        else:
            send(box, fwd_in.at[3], grad_send.at[13], grad_recv.at[12], me - 2, me >= e_slot)

    chunk(0)
    chunk(1)
    up(10)
    chunk(2)
    up(2)
    chunk(3)
    chunk(4)
    up(4)
    chunk(5)
    up(6)

    k8 = GROUP // 2
    take(partner_in.at[k8], grad_recv.at[k8], have, k8)
    take(fwd_in.at[3], grad_recv.at[12], have & (me + 2 < count), k8)
    take(far_in.at[1], grad_recv.at[15], have & is_odd & (me + 3 < count), k8)
    for k in (3, 2, 1):
        take(fwd_in.at[k - 1], grad_recv.at[8 + k], have & (chip - (k8 - k) >= 0), k8)
    outbox[SLOTS // 2 + k8] = part[k8].astype(jnp.bfloat16)
    send(outbox.at[SLOTS // 2 + k8], far_in.at[0], grad_send.at[14], grad_recv.at[13],
         me - GROUP, have)

    for h in range(heads):
        at = pl.ds(h * tok, tok)
        cols = pl.ds(h * hd, hd)
        att_buf[:, cols] = jnp.transpose(o_t[:, at]).astype(jnp.bfloat16)
        dq_buf[:, cols] = jnp.transpose(dq_t[:, at] * scale).astype(jnp.bfloat16)
    outs = [
        pltpu.make_async_copy(att_buf, attended, out_sem.at[0]),
        pltpu.make_async_copy(dq_buf, grad_query, out_sem.at[1]),
    ]
    for copy in outs:
        copy.start()

    take(partner_in.at[0], grad_recv.at[0], is_even, 0)
    for k in range(1, chips):
        take(own_in.at[k - 1], grad_recv.at[5 + k], chip + k < chips, 0)
    take(far_in.at[0], grad_recv.at[13], me + GROUP < count, 0)
    dkv_buf[...] = part[0].astype(jnp.bfloat16)
    last = [
        pltpu.make_async_copy(dkv_buf.at[0], grad_key, out_sem.at[2]),
        pltpu.make_async_copy(dkv_buf.at[1], grad_value, out_sem.at[3]),
    ]
    for copy in last:
        copy.start()
    for copy, there in sent:
        @pl.when(there)
        def _(copy=copy):
            copy.wait_send()
    for copy in outs + last:
        copy.wait()


def body(count, query, key, value, out_grad, lengths):
    tok, hd = key.shape
    heads = query.shape[1] // hd
    rows = heads * tok
    half = SLOTS // 2
    any_space = pl.BlockSpec(memory_space=pl.ANY)
    f32, bf16 = jnp.float32, jnp.bfloat16
    dma = pltpu.SemaphoreType.DMA
    scratch = [
        pltpu.VMEM((rows, hd), bf16),
        pltpu.VMEM((rows, hd), bf16),
        pltpu.VMEM((hd, rows), f32),
        pltpu.VMEM((SLOTS, 2, tok, hd), bf16),
        pltpu.VMEM((SLOTS, tok, rows), f32),
        pltpu.VMEM((SLOTS, tok, rows), f32),
        pltpu.VMEM((SLOTS, 1, rows), f32),
        pltpu.VMEM((1, rows), f32),
        pltpu.VMEM((1, rows), f32),
        pltpu.VMEM((hd, rows), f32),
        pltpu.VMEM((hd, rows), f32),
        pltpu.VMEM((half, 2, tok, hd), f32),
        pltpu.VMEM((2 * half, 2, tok, hd), bf16),
        pltpu.VMEM((half, 2, tok, hd), bf16),
        pltpu.VMEM((3, 2, tok, hd), bf16),
        pltpu.VMEM((4, 2, tok, hd), bf16),
        pltpu.VMEM((2, 2, tok, hd), bf16),
        pltpu.VMEM((tok, rows * hd // tok), bf16),
        pltpu.VMEM((tok, rows * hd // tok), bf16),
        pltpu.VMEM((2, tok, hd), bf16),
        dma((2 + 2 * heads,)),
        dma((SLOTS,)),
        dma((24,)),
        dma((16,)),
        dma((16,)),
        dma((4,)),
    ]
    return pl.pallas_call(
        functools.partial(kernel, count),
        out_shape=[
            jax.ShapeDtypeStruct(query.shape, bf16),
            jax.ShapeDtypeStruct(query.shape, bf16),
            jax.ShapeDtypeStruct(key.shape, bf16),
            jax.ShapeDtypeStruct(key.shape, bf16),
        ],
        in_specs=[pl.BlockSpec(memory_space=pltpu.SMEM)] + [any_space] * 4,
        out_specs=[any_space] * 4,
        scratch_shapes=scratch,
        compiler_params=pltpu.CompilerParams(
            collective_id=0, has_side_effects=True, vmem_limit_bytes=40 * 1024 * 1024),
        name="packed_attention",
    )(lengths, query, key, value, out_grad)


def solution(mesh):
    count = mesh.shape["ctx"]
    row = P("ctx", None)
    return jax.shard_map(
        functools.partial(body, count),
        mesh=mesh,
        in_specs=(row, row, row, row, P()),
        out_specs=(row, row, row, row),
        check_vma=False,
    )
```

time: 91.6 us -> 37.9 us (0.41)
  the two profiles are of different devices: /device:TPU:21 before, /device:TPU:10 now
where the time goes in v1:
time: 37.9 us; the launch traced here: 37.5 us
  Pallas kernels  30.2 us (80%)
  local copies, waits for them, and re-layouts  6.7 us (18%)
  between operations  0.65 us (2%)
    pallas_call x1, Pallas kernels, body(): pl.pallas_call(functools.partial(kernel, count), out_shape=[jax.ShapeDtyp...  30.2 us
    unnamed x14, local copies, waits for them, and re-layouts  6.7 us

profile of v1, /device:TPU:10, one launch (start us, length us, event | category | flops | bytes accessed | tf_op | source)
XLA Modules:
  0.0 37.5 jit_solution(10335775242829748752)
XLA Ops:
  0.6 0.0 copy-start
  0.6 0.9 %copy-done = bf16[128,1024]{1,0:T(8,128)(2,1)S(1)} copy-done((bf16[128,1024]{1,0:T(8,128)(2,1)S(1)}, bf16[128,1024]{1,0:T(8,128)(2,1)}, u32[]{:S(2)}) %copy-start) | copy-done | bytes 262168
  1.6 0.0 copy-start.1
  1.6 0.9 %copy-done.1 = bf16[128,1024]{1,0:T(8,128)(2,1)S(1)} copy-done((bf16[128,1024]{1,0:T(8,128)(2,1)S(1)}, bf16[128,1024]{1,0:T(8,128)(2,1)}, u32[]{:S(2)}) %copy-start.1) | copy-done | bytes 262168
  2.5 0.0 copy-start.2
  2.5 0.8 %copy-done.2 = bf16[128,128]{1,0:T(8,128)(2,1)S(1)} copy-done((bf16[128,128]{1,0:T(8,128)(2,1)S(1)}, bf16[128,128]{1,0:T(8,128)(2,1)}, u32[]{:S(2)}) %copy-start.2) | copy-done | bytes 32792
  3.3 0.0 copy-start.3
  3.3 0.8 %copy-done.3 = bf16[128,128]{1,0:T(8,128)(2,1)S(1)} copy-done((bf16[128,128]{1,0:T(8,128)(2,1)S(1)}, bf16[128,128]{1,0:T(8,128)(2,1)}, u32[]{:S(2)}) %copy-start.3) | copy-done | bytes 32792
  4.1 0.0 copy-start.4
  4.1 0.7 %copy-done.4 = s32[32]{0:T(128)S(1)} copy-done((s32[32]{0:T(128)S(1)}, s32[32]{0:T(128)}, u32[]{:S(2)}) %copy-start.4) | copy-done | bytes 152
  4.7 30.2 %packed_attention.1 = (bf16[128,1024]{1,0:T(8,128)(2,1)S(1)}, bf16[128,1024]{1,0:T(8,128)(2,1)S(1)}, bf16[128,128]{1,0:T(8,128)(2,1)S(1)}, bf16[128,128]{1,0:T(8,128)(2,1)S(1)}) custom-call(s32[32]{0:T(128)S(1)} %copy-done.4, bf16[128,1024]{1,0:T(8,128)(2,1)S(1)} %copy-done, bf16[128,128]{1,0:T(8,128)(2,1)S(1)} %copy-done.2, bf16[128,128]{1,0:T(8,128)(2,1)S(1)} %copy-done.3, ...), custom_call_target="tpu_custom_call" | custom-call | tf_op jit(solution)/shard_map/packed_attention/pallas_call | solution.py:354
  34.9 0.7 %copy.13 = bf16[128,1024]{1,0:T(8,128)(2,1)} copy(bf16[128,1024]{1,0:T(8,128)(2,1)S(1)} %get-tuple-element.8) | data formatting | bytes 524288
  35.6 0.7 %copy.14 = bf16[128,1024]{1,0:T(8,128)(2,1)} copy(bf16[128,1024]{1,0:T(8,128)(2,1)S(1)} %get-tuple-element.9) | data formatting | bytes 524288
  36.3 0.6 %copy.15 = bf16[128,128]{1,0:T(8,128)(2,1)} copy(bf16[128,128]{1,0:T(8,128)(2,1)S(1)} %get-tuple-element.10) | data formatting | bytes 65536
  36.9 0.6 %copy.16 = bf16[128,128]{1,0:T(8,128)(2,1)} copy(bf16[128,128]{1,0:T(8,128)(2,1)S(1)} %get-tuple-element.11) | data formatting | bytes 65536
Async XLA Ops:
  0.6 1.0 %copy-start = (bf16[128,1024]{1,0:T(8,128)(2,1)S(1)}, bf16[128,1024]{1,0:T(8,128)(2,1)}, u32[]{:S(2)}) copy-start(bf16[128,1024]{1,0:T(8,128)(2,1)} %query.1) | copy-start | bytes 786436
  1.6 0.9 %copy-start.1 = (bf16[128,1024]{1,0:T(8,128)(2,1)S(1)}, bf16[128,1024]{1,0:T(8,128)(2,1)}, u32[]{:S(2)}) copy-start(bf16[128,1024]{1,0:T(8,128)(2,1)} %out_grad.1) | copy-start | bytes 786436
  2.5 0.8 %copy-start.2 = (bf16[128,128]{1,0:T(8,128)(2,1)S(1)}, bf16[128,128]{1,0:T(8,128)(2,1)}, u32[]{:S(2)}) copy-start(bf16[128,128]{1,0:T(8,128)(2,1)} %key.1) | copy-start | bytes 98308
  3.3 0.8 %copy-start.3 = (bf16[128,128]{1,0:T(8,128)(2,1)S(1)}, bf16[128,128]{1,0:T(8,128)(2,1)}, u32[]{:S(2)}) copy-start(bf16[128,128]{1,0:T(8,128)(2,1)} %value.1) | copy-start | bytes 98308
  4.1 0.7 %copy-start.4 = (s32[32]{0:T(128)S(1)}, s32[32]{0:T(128)}, u32[]{:S(2)}) copy-start(s32[32]{0:T(128)} %lengths.1) | copy-start | bytes 388

commit v2 on v1

--- a/solution.py
+++ b/solution.py
@@ -26,8 +26,8 @@
     lengths, query, key, value, out_grad,
     attended, grad_query, grad_key, grad_value,
     q, g, g_t, kv, e_all, dp_all, m_slot, m_run, l_run, o_t, dq_t,
-    part, outbox, partner_in, own_in, fwd_in, far_in, att_buf, dq_buf, dkv_buf,
-    load_sem, recv_sem, send_sem, grad_recv, grad_send, out_sem,
+    part, outbox, partner_in, own_in, fwd_in, far_in,
+    load_sem, recv_sem, send_sem, grad_recv, grad_send,
 ):
     tok = key.shape[0]
     hd = key.shape[1]
@@ -287,31 +287,29 @@
     for h in range(heads):
         at = pl.ds(h * tok, tok)
         cols = pl.ds(h * hd, hd)
-        att_buf[:, cols] = jnp.transpose(o_t[:, at]).astype(jnp.bfloat16)
-        dq_buf[:, cols] = jnp.transpose(dq_t[:, at] * scale).astype(jnp.bfloat16)
-    outs = [
-        pltpu.make_async_copy(att_buf, attended, out_sem.at[0]),
-        pltpu.make_async_copy(dq_buf, grad_query, out_sem.at[1]),
-    ]
-    for copy in outs:
-        copy.start()
+        attended[:, cols] = jnp.transpose(o_t[:, at]).astype(jnp.bfloat16)
+        grad_query[:, cols] = jnp.transpose(dq_t[:, at] * scale).astype(jnp.bfloat16)
 
     take(partner_in.at[0], grad_recv.at[0], is_even, 0)
     for k in range(1, chips):
         take(own_in.at[k - 1], grad_recv.at[5 + k], chip + k < chips, 0)
     take(far_in.at[0], grad_recv.at[13], me + GROUP < count, 0)
-    dkv_buf[...] = part[0].astype(jnp.bfloat16)
-    last = [
-        pltpu.make_async_copy(dkv_buf.at[0], grad_key, out_sem.at[2]),
-        pltpu.make_async_copy(dkv_buf.at[1], grad_value, out_sem.at[3]),
-    ]
-    for copy in last:
-        copy.start()
+    grad_key[...] = part[0, 0].astype(jnp.bfloat16)
+    grad_value[...] = part[0, 1].astype(jnp.bfloat16)
     for copy, there in sent:
         @pl.when(there)
         def _(copy=copy):
             copy.wait_send()
-    for copy in outs + last:
+
+
+def write_out(a, b, c, d, a_out, b_out, c_out, d_out, sem):
+    copies = [
+        pltpu.make_async_copy(src, dst, sem.at[i])
+        for i, (src, dst) in enumerate(((a, a_out), (b, b_out), (c, c_out), (d, d_out)))
+    ]
+    for copy in copies:
+        copy.start()
+    for copy in copies:
         copy.wait()
 
 
@@ -320,7 +318,7 @@
     heads = query.shape[1] // hd
     rows = heads * tok
     half = SLOTS // 2
-    any_space = pl.BlockSpec(memory_space=pl.ANY)
+    in_hbm = pl.BlockSpec(memory_space=pltpu.HBM)
     f32, bf16 = jnp.float32, jnp.bfloat16
     dma = pltpu.SemaphoreType.DMA
     scratch = [
@@ -341,17 +339,15 @@
         pltpu.VMEM((3, 2, tok, hd), bf16),
         pltpu.VMEM((4, 2, tok, hd), bf16),
         pltpu.VMEM((2, 2, tok, hd), bf16),
-        pltpu.VMEM((tok, rows * hd // tok), bf16),
-        pltpu.VMEM((tok, rows * hd // tok), bf16),
-        pltpu.VMEM((2, tok, hd), bf16),
         dma((2 + 2 * heads,)),
         dma((SLOTS,)),
         dma((24,)),
         dma((16,)),
         dma((16,)),
-        dma((4,)),
     ]
-    return pl.pallas_call(
+    query, key, value, out_grad = [
+        pltpu.with_memory_space_constraint(x, pltpu.HBM) for x in (query, key, value, out_grad)]
+    results = pl.pallas_call(
         functools.partial(kernel, count),
         out_shape=[
             jax.ShapeDtypeStruct(query.shape, bf16),
@@ -359,13 +355,22 @@
             jax.ShapeDtypeStruct(key.shape, bf16),
             jax.ShapeDtypeStruct(key.shape, bf16),
         ],
-        in_specs=[pl.BlockSpec(memory_space=pltpu.SMEM)] + [any_space] * 4,
-        out_specs=[any_space] * 4,
+        in_specs=[pl.BlockSpec(memory_space=pltpu.SMEM)] + [in_hbm] * 4,
+        out_specs=[pl.BlockSpec(memory_space=pltpu.VMEM)] * 4,
         scratch_shapes=scratch,
         compiler_params=pltpu.CompilerParams(
             collective_id=0, has_side_effects=True, vmem_limit_bytes=40 * 1024 * 1024),
         name="packed_attention",
     )(lengths, query, key, value, out_grad)
+    results = [pltpu.with_memory_space_constraint(x, pltpu.VMEM) for x in results]
+    return pl.pallas_call(
+        write_out,
+        out_shape=[jax.ShapeDtypeStruct(r.shape, r.dtype) for r in results],
+        in_specs=[pl.BlockSpec(memory_space=pl.ANY)] * 4,
+        out_specs=[in_hbm] * 4,
+        scratch_shapes=[dma((4,))],
+        name="write_out",
+    )(*results)
 
 
 def solution(mesh):

time: 37.9 us -> 32.2 us (0.85)
  local copies, waits for them, and re-layouts: 6.7 us -> 0.65 us
  Pallas kernels: 30.2 us -> 30.7 us
    unnamed x14 -> x2, local copies, waits for them, and re-layouts: 6.7 us -> 0.65 us
    pallas_call x0 -> x1, Pallas kernels: none -> 0.84 us  [body(): pl.pallas_call(write_out, out_shape=[jax.ShapeDtypeStruct(r.shape, r.dtyp...]
where the time goes in v2:
time: 32.2 us; the launch traced here: 32 us
  Pallas kernels  30.7 us (95%)
  local copies, waits for them, and re-layouts  0.65 us (2%)
  between operations  0.65 us (2%)
    pallas_call x1, Pallas kernels, body(): pl.pallas_call(functools.partial(kernel, count), out_shape=[jax.ShapeDtyp...  29.8 us
    pallas_call x1, Pallas kernels, body(): pl.pallas_call(write_out, out_shape=[jax.ShapeDtypeStruct(r.shape, r.dtyp...  0.84 us
    unnamed x2, local copies, waits for them, and re-layouts  0.65 us

profile of v2, /device:TPU:10, one launch (start us, length us, event | category | flops | bytes accessed | tf_op | source)
XLA Modules:
  0.0 32.0 jit_solution(2402672928534980119)
XLA Ops:
  0.6 0.0 copy-start
  0.6 0.6 %copy-done = s32[32]{0:T(128)S(1)} copy-done((s32[32]{0:T(128)S(1)}, s32[32]{0:T(128)}, u32[]{:S(2)}) %copy-start) | copy-done | bytes 152
  1.3 29.8 %packed_attention.1 = (bf16[128,1024]{1,0:T(8,128)(2,1)S(1)}, bf16[128,1024]{1,0:T(8,128)(2,1)S(1)}, bf16[128,128]{1,0:T(8,128)(2,1)S(1)}, bf16[128,128]{1,0:T(8,128)(2,1)S(1)}) custom-call(s32[32]{0:T(128)S(1)} %copy-done, bf16[128,1024]{1,0:T(8,128)(2,1)} %query.1, bf16[128,128]{1,0:T(8,128)(2,1)} %key.1, bf16[128,128]{1,0:T(8,128)(2,1)} %value.1, ...), custom_call_target="tpu_custom_call" | custom-call | tf_op jit(solution)/shard_map/packed_attention/pallas_call | solution.py:350
  31.1 0.8 %write_out.1 = (bf16[128,1024]{1,0:T(8,128)(2,1)}, bf16[128,1024]{1,0:T(8,128)(2,1)}, bf16[128,128]{1,0:T(8,128)(2,1)}, bf16[128,128]{1,0:T(8,128)(2,1)}) custom-call(bf16[128,1024]{1,0:T(8,128)(2,1)S(1)} %get-tuple-element.8.a, bf16[128,1024]{1,0:T(8,128)(2,1)S(1)} %get-tuple-element.9.b, bf16[128,128]{1,0:T(8,128)(2,1)S(1)} %get-tuple-element.10.c, ...), custom_call_target="tpu_custom_call" | custom-call | tf_op jit(solution)/shard_map/write_out/pallas_call | solution.py:366
Async XLA Ops:
  0.6 0.7 %copy-start = (s32[32]{0:T(128)S(1)}, s32[32]{0:T(128)}, u32[]{:S(2)}) copy-start(s32[32]{0:T(128)} %lengths.1) | copy-start | bytes 388
